TPU v7x, 128 devices: a whole 4x4x4 slice. The times are simulated.
128 devices in a mesh: row: 8 (over z, core), col: 16 (over x, y).
Axes of the slice: x: 4, y: 4, z: 4, core: 2. Of those that a mesh axis runs over, the one named last changes fastest.
Arguments:
- hamiltonian: bfloat16 [4096, 4096], P('row', 'col'), may hold values from -0.3 to 0.3
- pattern: int32 [32, 32], replicated, may hold values from 0 to 1, as said below
- tile_lists: int32 [128, 8], replicated, may hold values from 0 to 31, as said below
- orders: int32 [128], replicated, may hold values from 6 to 8
- shift: float32 [1], replicated, may hold values from -0.5 to 0.5
Outputs:
- density: bfloat16 [4096, 4096], P('row', 'col')
- php: float32 [4096, 4096], P('row', 'col')
Inputs may be any that keep to these rules, and one draw needn't show every extreme that they name: `pattern`: Symmetric, with zeros on the diagonal. `tile_lists`: row s begins with tile s * 32 // 128; its entries lie in distinct groups of 2 consecutive tiles, and the second lies in the group that shares a group of 4 consecutive tiles with the first. Entries from position orders[s] on are not used.
All inputs are finite; a program needn't handle non-finite values.
Results may differ from a plain program's by a relative error of at most 0.0073.
Values may be sent and summed in bfloat16 or wider, within the bound.
No kernel may reach another device: no remote copies, remote signals or barrier semaphores. Data moves between devices by JAX's collectives and lax.ppermute only.
A program may use at most 64 MiB of HBM per device.

v0:
```python
import jax
import jax.numpy as jnp
from jax import lax
from jax.sharding import Mesh
from jax.sharding import PartitionSpec as P

TILE = 128
TPC = 2
MAXT = 8
ITERS = 3
COL = ("col_0", "col_1")
ROW_COL = ("row", "col_0", "col_1")


def sent_to_all(x, axis):
    size = lax.axis_size(axis)
    return lax.all_to_all(jnp.broadcast_to(x[None], (size, *x.shape)), axis, 0, 0, tiled=True)


def joined_along(parts, dim):
    parts = jnp.moveaxis(parts, 0, dim)
    lengths = parts.shape
    return parts.reshape(*lengths[:dim], lengths[dim] * lengths[dim + 1], *lengths[dim + 2 :])


def collect(x, axis, dim):
    parts = sent_to_all(x, axis)
    return joined_along(parts, dim)


def gather_axes(x, axes, dim):
    result = x
    for number in range(len(axes) - 1, -1, -1):
        result = lax.all_gather(result, axes[number], axis=dim, tiled=True)
    return result


def newton_density(sub, live_rows, potential):
    eye = jnp.eye(sub.shape[0], dtype=jnp.float32)
    shifted = sub.astype(jnp.float32) - potential * eye * live_rows[None, :]
    row_squares = jnp.sum(shifted * shifted, axis=1)
    scale = jnp.abs(potential) + 2.0 * jnp.sqrt(jnp.max(row_squares) + 1e-06)
    iterate = (shifted / scale).astype(jnp.bfloat16)
    product = shifted
    for step in range(ITERS):
        square = jnp.dot(iterate, iterate, preferred_element_type=jnp.float32)
        factor = (1.5 * eye - 0.5 * square).astype(jnp.bfloat16)
        product = jnp.dot(iterate, factor, preferred_element_type=jnp.float32)
        if step + 1 < ITERS:
            iterate = product.astype(jnp.bfloat16)
    return 0.5 * (eye - product)


def per_device(hamiltonian, pattern, tile_lists, orders, shift):
    rows_n = lax.axis_size("row")
    cols_n = lax.axis_size(COL)
    devices = rows_n * cols_n
    me_row = lax.axis_index("row")
    me_col = lax.axis_index(COL)
    solver = me_row * cols_n + me_col
    count = pattern.shape[0]
    row_tiles = count // rows_n
    width = TPC * TILE // rows_n
    pairs = MAXT * MAXT
    steps = jnp.arange(MAXT, dtype=jnp.int32)
    keep = jnp.maximum(pattern, jnp.eye(count, dtype=jnp.int32))
    local_keep = lax.dynamic_slice(keep, (me_row * row_tiles, me_col * TPC), (row_tiles, TPC))
    full_keep = jnp.repeat(jnp.repeat(local_keep, TILE, axis=0), TILE, axis=1)
    masked = jnp.where(full_keep > 0, hamiltonian, jnp.zeros_like(hamiltonian))
    blocks = (
        masked.reshape(row_tiles, TILE, TPC, TILE)
        .transpose(0, 2, 1, 3)
        .reshape(row_tiles * TPC, TILE, TILE)
    )
    live_all = steps[None, :] < orders[:, None]
    owned = (tile_lists[:, :, None] // row_tiles == me_row) & (
        tile_lists[:, None, :] // TPC == me_col
    )
    owned = owned & live_all[:, :, None] & live_all[:, None, :]
    owned = owned.reshape(devices, pairs)
    rank = jnp.cumsum(owned.astype(jnp.int32), axis=1) - 1
    local_index = (
        (tile_lists[:, :, None] - me_row * row_tiles) * TPC
        + (tile_lists[:, None, :] - me_col * TPC)
    ).reshape(devices, pairs)
    slots = []
    for slot in range(2):
        pick = owned & (rank == slot)
        found = jnp.any(pick, axis=1)
        which = jnp.sum(jnp.where(pick, local_index, 0), axis=1)
        picked = jnp.take(blocks, which, axis=0)
        slots.append(jnp.where(found[:, None, None], picked, jnp.zeros_like(picked)))
    outgoing = jnp.stack(slots, axis=1)
    arrived = lax.all_to_all(outgoing, ROW_COL, split_axis=0, concat_axis=0, tiled=True)
    arrived = arrived.reshape(devices * 2, TILE, TILE)
    mine = lax.dynamic_index_in_dim(tile_lists, solver, 0, keepdims=False)
    order_here = lax.dynamic_index_in_dim(orders, solver, 0, keepdims=False)
    live = steps < order_here
    both = (live[:, None] & live[None, :]).reshape(pairs)
    owner = (mine[:, None] // row_tiles * cols_n + mine[None, :] // TPC).reshape(pairs)
    flat_pairs = jnp.arange(pairs, dtype=jnp.int32)
    earlier = (
        (owner[:, None] == owner[None, :])
        & both[None, :]
        & (flat_pairs[None, :] < flat_pairs[:, None])
    )
    slot_of = jnp.sum(earlier.astype(jnp.int32), axis=1)
    source = jnp.where(both, owner * 2 + slot_of, 0)
    sub = jnp.take(arrived, source, axis=0)
    sub = jnp.where(both[:, None, None], sub, jnp.zeros_like(sub))
    sub = (
        sub.reshape(MAXT, MAXT, TILE, TILE).transpose(0, 2, 1, 3).reshape(MAXT * TILE, MAXT * TILE)
    )
    live_rows = jnp.repeat(live.astype(jnp.float32), TILE)
    dens = newton_density(sub, live_rows, shift[0])
    offset = solver * width % TILE
    central = lax.dynamic_slice_in_dim(dens, offset, width, 1).astype(jnp.bfloat16)
    central = central.reshape(MAXT, TILE, width).transpose(0, 2, 1)
    home_col = solver * width // (TPC * TILE)
    groups = mine // row_tiles
    ahead = (groups[:, None] == groups[None, :]) & live[None, :] & (steps[None, :] < steps[:, None])
    place = jnp.sum(ahead.astype(jnp.int32), axis=1)
    target = groups * cols_n + home_col
    chooser = jnp.arange(devices, dtype=jnp.int32)[:, None, None] == target[None, None, :]
    chooser = (
        chooser
        & (jnp.arange(2, dtype=jnp.int32)[None, :, None] == place[None, None, :])
        & live[None, None, :]
    )
    back = jnp.einsum(
        "dki,iwt->dkwt", chooser.astype(jnp.bfloat16), central, preferred_element_type=jnp.float32
    ).astype(jnp.bfloat16)
    returned = lax.all_to_all(back, ROW_COL, split_axis=0, concat_axis=0, tiled=True)
    returned = returned.reshape(devices * 2, width, TILE)
    homes = lax.dynamic_slice_in_dim(tile_lists, me_col * rows_n, rows_n, 0)
    home_orders = lax.dynamic_slice_in_dim(orders, me_col * rows_n, rows_n, 0)
    home_live = steps[None, :] < home_orders[:, None]
    home_groups = homes // row_tiles
    home_ahead = (
        (home_groups[:, :, None] == home_groups[:, None, :])
        & home_live[:, None, :]
        & (steps[None, None, :] < steps[None, :, None])
    )
    home_place = jnp.sum(home_ahead.astype(jnp.int32), axis=2)
    local_rows = me_row * row_tiles + jnp.arange(row_tiles, dtype=jnp.int32)
    hit = (homes[None, :, :] == local_rows[:, None, None]) & home_live[None, :, :]
    found = jnp.any(hit, axis=2)
    slot_here = jnp.sum(jnp.where(hit, home_place[None, :, :], 0), axis=2)
    sub_index = me_col * rows_n + jnp.arange(rows_n, dtype=jnp.int32)
    flat_index = jnp.where(found, sub_index[None, :] * 2 + slot_here, 0)
    pieces = jnp.take(returned, flat_index.reshape(-1), axis=0).reshape(
        row_tiles, rows_n, width, TILE
    )
    pieces = jnp.where(found[:, :, None, None], pieces, jnp.zeros_like(pieces))
    density = pieces.transpose(0, 3, 1, 2).reshape(row_tiles * TILE, rows_n * width)
    p_strip = collect(density, "row", 0)
    part = p_strip
    hp = jnp.dot(gather_axes(masked, COL, 1), part, preferred_element_type=jnp.float32).astype(
        jnp.bfloat16
    )
    q_strip = collect(hp, "row", 0)
    part = q_strip
    php = jnp.dot(
        lax.all_gather(density, COL, axis=1, tiled=True), part, preferred_element_type=jnp.float32
    )
    return (density, php)


def solution(mesh):
    split = Mesh(mesh.devices.reshape(mesh.shape["row"], 4, 4), ("row", "col_0", "col_1"))
    placed = (P("row", COL), P(), P(), P(), P())
    return jax.shard_map(
        per_device,
        mesh=split,
        in_specs=placed,
        out_specs=(P("row", COL), P("row", COL)),
        check_vma=False,
    )
```

profile of v0, /device:TPU:1, one launch (start us, length us, event | category | flops | bytes accessed | tf_op | source)
XLA Modules:
  0.0 318.0 jit_solution(3144820847823193757)
XLA Ops:
  7.2 0.7 fusion.33
  7.9 0.7 subtract_multiply_fusion
  8.6 0.7 iota_compare_fusion.2
  9.2 0.1 reduce_window_sum.11
  9.4 0.8 fusion.44
  10.2 0.1 copy.47
  10.3 0.1 broadcast_bitcast_fusion.1
  10.4 1.1 copy.48
  11.6 0.2 copy.49
  11.9 3.1 gather_fusion.2
  14.9 3.0 gather_fusion.3
  17.9 2.9 fusion.6
  20.8 0.6 copy-done
  21.4 2.4 fusion.5
  23.8 6.2 %pad_maximum_fusion = bf16[128,2,128,128]{3,2,0,1:T(8,128)(2,1)} fusion(bf16[128,1,128,128]{3,2,0,1:T(8,128)(2,1)} %fusion.5, bf16[128,1,128,128]{3,2,0,1:T(8,128)(2,1)S(1)} %fusion.6), kind=kLoop, calls=%fused_computation.4 | loop fusion | flops 4194304 | bytes 16777216 | tf_op jit(solution)/shard_map/stack | solution.py:93
  30.0 10.3 %copy.50 = bf16[128,2,128,128]{3,2,1,0:T(8,128)(2,1)} copy(bf16[128,2,128,128]{3,2,0,1:T(8,128)(2,1)} %pad_maximum_fusion) | data formatting | bytes 16777216 | tf_op jit(solution)/shard_map/stack | solution.py:93
  40.3 11.9 %all-to-all-start = ((bf16[128,2,128,128]{3,2,1,0:T(8,128)(2,1)}), bf16[128,2,128,128]{3,2,1,0:T(8,128)(2,1)}, u32[]{:S(2)}, u32[]{:S(2)}) async-start(bf16[128,2,128,128]{3,2,1,0:T(8,128)(2,1)} %copy.50), calls=%async_computation | async-start | bytes 16777216 | tf_op jit(solution)/shard_map/all_to_all | solution.py:94
  52.3 0.7 all-gather.6.cloned.1.call-update
  53.1 0.6 dynamic_slice.23
  53.7 0.2 fusion.29
  53.9 0.7 iota_compare_fusion.7
  54.6 0.2 broadcast_multiply_fusion
  54.8 0.1 add.281
  54.9 0.1 and.325
  55.0 0.2 convert_reduce_fusion
  55.2 0.7 fusion.57
  55.9 0.1 and.342
  56.0 0.1 mul.129
  56.8 0.3 iota_compare_fusion
  57.3 0.1 compare_and_fusion.1
  57.4 93.7 %all-gather.6.cloned.1.call-done = bf16[512,1024]{0,1:T(8,128)(2,1)} async-done(((bf16[512,256]{0,1:T(8,128)(2,1)}), bf16[512,1024]{0,1:T(8,128)(2,1)}) %all-gather.6.cloned.1.call-update) | async-done | bytes 1048592 | tf_op jit(solution)/shard_map/all_gather | solution.py:34
  151.1 6.7 %all-to-all-done = bf16[128,2,128,128]{3,2,1,0:T(8,128)(2,1)} async-done(((bf16[128,2,128,128]{3,2,1,0:T(8,128)(2,1)}), bf16[128,2,128,128]{3,2,1,0:T(8,128)(2,1)}, u32[]{:S(2)}, u32[]{:S(2)}) %all-to-all-start) | async-done | bytes 8388640 | tf_op jit(solution)/shard_map/all_to_all | solution.py:94
  157.9 4.3 %gather_fusion = bf16[64,128,128]{2,1,0:T(8,128)(2,1)S(1)} fusion(bf16[256,128,128]{2,1,0:T(8,128)(2,1)} %bitcast.11, s32[1024]{0:T(1024)S(1)} %pad_clamp_fusion.1), kind=kCustom, calls=%fused_computation.2 | custom fusion | bytes 4194560 | tf_op jit(solution)/shard_map/jit(_take)/gather | solution.py:109
  162.2 1.7 multiply_reduce_fusion
  164.0 0.6 reduce_max.9
  165.3 1.8 divide_convert_fusion
  167.1 0.4 convert_bitcast_fusion
  167.5 1.4 copy.52
  168.9 4.3 %copy.51 = f32[8,128,8,128]{3,2,1,0:T(8,128)} copy(f32[8,128,8,128]{3,1,2,0:T(8,128)S(1)} %convert_bitcast_fusion) | data formatting | bytes 8388608 | tf_op jit(solution)/shard_map/convert_element_type | solution.py:40
  173.2 8.2 %fusion.11 = bf16[1024,1024]{1,0:T(8,128)(2,1)} fusion(f32[128,8,8,128]{3,2,1,0:T(8,128)} %bitcast.114, f32[]{:T(128)S(6)} %add.295, f32[1024]{0:T(1024)S(1)} %broadcast_bitcast_fusion, f32[]{:T(128)} %bitcast.107, bf16[128,8,8,128]{3,2,1,0:T(8,128)(2,1)S(1)} %bitcast.119), kind=kOutput, calls=%fused_computation.27 | convolution fusion | flops 4307550208 | bytes 8392712 | tf_op jit(solution)/shard_map/dot_general | solution.py:48
  181.4 7.4 %convolution_convert_fusion.1 = bf16[1024,1024]{1,0:T(8,128)(2,1)S(1)} fusion(bf16[1024,1024]{1,0:T(8,128)(2,1)} %fusion.11), kind=kOutput, calls=%fused_computation.29 | convolution fusion | flops 4301258752 | bytes 4194304 | tf_op jit(solution)/shard_map/dot_general | solution.py:48
  188.8 6.7 %fusion.16 = f32[1024,1024]{1,0:T(8,128)} fusion(bf16[1024,1024]{1,0:T(8,128)(2,1)S(1)} %convolution_convert_fusion.1), kind=kOutput, calls=%fused_computation.31 | convolution fusion | flops 4300210176 | bytes 6291456 | tf_op jit(solution)/shard_map/dot_general | solution.py:48
  195.5 1.4 fusion.18
  196.9 0.1 copy.54
  197.0 0.8 convolution_convert_fusion
  197.8 2.7 copy.55
  200.5 8.4 %all-to-all-start.1 = ((bf16[128,2,32,128]{3,2,1,0:T(8,128)(2,1)}), bf16[128,2,32,128]{3,2,1,0:T(8,128)(2,1)S(1)}, u32[]{:S(2)}, u32[]{:S(2)}) async-start(bf16[128,2,32,128]{3,2,1,0:T(8,128)(2,1)} %copy.55), calls=%async_computation.1 | async-start | bytes 4194304 | tf_op jit(solution)/shard_map/all_to_all | solution.py:133
  209.3 0.2 fusion.23
  209.6 0.3 convert_reduce_fusion.1
  209.8 0.2 select_reduce_fusion
  210.1 0.1 select_n.226
  210.2 28.5 %all-to-all-done.1 = bf16[128,2,32,128]{3,2,1,0:T(8,128)(2,1)S(1)} async-done(((bf16[128,2,32,128]{3,2,1,0:T(8,128)(2,1)}), bf16[128,2,32,128]{3,2,1,0:T(8,128)(2,1)S(1)}, u32[]{:S(2)}, u32[]{:S(2)}) %all-to-all-start.1) | async-done | bytes 2097184 | tf_op jit(solution)/shard_map/all_to_all | solution.py:133
  238.7 0.6 gather_fusion.1
  239.3 0.1 select_bitcast_fusion
  239.4 0.2 copy.56
  239.7 0.7 copy.78
  240.4 1.1 copy.58
  241.5 1.5 broadcast_in_dim.170
  243.0 4.6 %all-to-all-start.2 = ((bf16[8,512,256]{2,1,0:T(8,128)(2,1)}), bf16[8,512,256]{2,1,0:T(8,128)(2,1)S(1)}, u32[]{:S(2)}, u32[]{:S(2)}) async-start(bf16[8,512,256]{2,1,0:T(8,128)(2,1)} %broadcast_in_dim.170), calls=%async_computation.2 | async-start | bytes 4194304 | tf_op jit(solution)/shard_map/all_to_all | solution.py:17
  247.6 26.2 %all-to-all-done.2 = bf16[8,512,256]{2,1,0:T(8,128)(2,1)S(1)} async-done(((bf16[8,512,256]{2,1,0:T(8,128)(2,1)}), bf16[8,512,256]{2,1,0:T(8,128)(2,1)S(1)}, u32[]{:S(2)}, u32[]{:S(2)}) %all-to-all-start.2) | async-done | bytes 2097184 | tf_op jit(solution)/shard_map/all_to_all | solution.py:17
  273.8 3.6 %convolution_convert_fusion.2 = bf16[512,256]{1,0:T(8,128)(2,1)S(1)} fusion(bf16[512,4096]{0,1:T(8,128)(2,1)} %all-gather.8.cloned.1.call-done, bf16[4096,256]{1,0:T(8,128)(2,1)S(1)} %bitcast.118), kind=kOutput, calls=%fused_computation.30 | convolution fusion | flops 1073872896 | bytes 6553600 | tf_op jit(solution)/shard_map/dot_general | solution.py:158
  277.4 0.1 broadcast_in_dim.171
  277.6 29.6 %all_to_all.20 = bf16[8,512,256]{2,1,0:T(8,128)(2,1)S(1)} all-to-all(bf16[8,512,256]{2,1,0:T(8,128)(2,1)S(1)} %broadcast_in_dim.171), channel_id=1, replica_groups=mesh['row'=8,'col_0'=4,'col_1'=4] {'row'}, dimensions={0} | all-to-all | bytes 4194304 | tf_op jit(solution)/shard_map/all_to_all | solution.py:17
  307.2 4.3 %fusion.60 = f32[512,256]{1,0:T(8,128)} fusion(bf16[512,4096]{0,1:T(8,128)(2,1)} %all-gather.4.cloned.1.call-done, bf16[4096,256]{1,0:T(8,128)(2,1)S(1)} %bitcast.120), kind=kOutput, calls=%fused_computation.155 | convolution fusion | flops 1073741824 | bytes 6815744 | tf_op jit(solution)/shard_map/dot_general | solution.py:163
  (47 shorter events, 1.1 us)
Async XLA Ops:
  11.5 3.4 %copy-start.1 = (bf16[512,256]{0,1:T(8,128)(2,1)}, bf16[512,256]{0,1:T(8,128)(2,1)S(1)}, u32[]{:S(2)}) copy-start(bf16[512,256]{0,1:T(8,128)(2,1)S(1)} %bitcast_select_fusion) | copy-start | bytes 786436
  17.9 3.4 %copy-start = (bf16[128,128,128]{2,1,0:T(8,128)(2,1)S(1)}, bf16[128,128,128]{2,1,0:T(8,128)(2,1)}, u32[]{:S(2)}) copy-start(bf16[128,128,128]{2,1,0:T(8,128)(2,1)} %gather_fusion.3) | copy-start | bytes 12582916
  40.3 12.8 %copy-start.4 = (s32[128]{0:T(128)S(1)}, s32[128]{0:T(128)}, u32[]{:S(2)}) copy-start(s32[128]{0:T(128)} %param.10) | copy-start | bytes 1540
  40.3 13.4 %copy-start.3 = (s32[128,8]{0,1:T(8,128)S(1)}, s32[128,8]{0,1:T(8,128)}, u32[]{:S(2)}) copy-start(s32[128,8]{0,1:T(8,128)} %param.9) | copy-start | bytes 12292
  40.3 117.6 %all-to-all-start = ((bf16[128,2,128,128]{3,2,1,0:T(8,128)(2,1)}), bf16[128,2,128,128]{3,2,1,0:T(8,128)(2,1)}, u32[]{:S(2)}, u32[]{:S(2)}) async-start(bf16[128,2,128,128]{3,2,1,0:T(8,128)(2,1)} %copy.50), calls=%async_computation | async-start | bytes 16777216 | tf_op jit(solution)/shard_map/all_to_all | solution.py:94
  52.3 98.8 %all-gather.6.cloned.1.call-start = ((), (), s32[]{:S(2)}) async-start(), calls=%async_computation.5 | async-start | bytes 1310720 | tf_op jit(solution)/shard_map/all_gather | solution.py:34
  53.0 194.6 %all-gather.8.cloned.1.call-start = ((), (), s32[]{:S(2)}) async-start(), calls=%async_computation.6 | async-start | bytes 5242880 | tf_op jit(solution)/shard_map/all_gather | solution.py:34
  200.5 38.2 %all-to-all-start.1 = ((bf16[128,2,32,128]{3,2,1,0:T(8,128)(2,1)}), bf16[128,2,32,128]{3,2,1,0:T(8,128)(2,1)S(1)}, u32[]{:S(2)}, u32[]{:S(2)}) async-start(bf16[128,2,32,128]{3,2,1,0:T(8,128)(2,1)} %copy.55), calls=%async_computation.1 | async-start | bytes 4194304 | tf_op jit(solution)/shard_map/all_to_all | solution.py:133
  209.0 98.2 %all-gather.4.cloned.1.call-start = ((), (), s32[]{:S(2)}) async-start(), calls=%async_computation.4 | async-start | bytes 4456448 | tf_op jit(solution)/shard_map/all_gather | solution.py:164
  241.5 35.9 %copy-start.2 = (bf16[512,256]{1,0:T(8,128)(2,1)}, bf16[512,256]{1,0:T(8,128)(2,1)S(1)}, u32[]{:S(2)}) copy-start(bf16[512,256]{1,0:T(8,128)(2,1)S(1)} %copy.58) | copy-start | bytes 786436
  243.0 30.9 %all-to-all-start.2 = ((bf16[8,512,256]{2,1,0:T(8,128)(2,1)}), bf16[8,512,256]{2,1,0:T(8,128)(2,1)S(1)}, u32[]{:S(2)}, u32[]{:S(2)}) async-start(bf16[8,512,256]{2,1,0:T(8,128)(2,1)} %broadcast_in_dim.170), calls=%async_computation.2 | async-start | bytes 4194304 | tf_op jit(solution)/shard_map/all_to_all | solution.py:17
Sparse Core Ops, SparseCore 0:
  55.3 95.7 all-gather.5
  152.8 50.1 all-gather.7
  240.5 47.3 all-gather.3
where the time goes:
time: 319 us; the launch traced here: 318 us
  waiting for transfers between devices  156 us (49%)
  local copies, waits for them, and re-layouts  37 us (12%)
  matrix products  30.9 us (10%)
  blocking collectives  29.6 us (9%)
  starting transfers between devices  25.1 us (8%)
  other arithmetic  23.9 us (7%)
  between operations  15.5 us (5%)
    all_gather x2, waiting for transfers between devices, gather_axes(): result = lax.all_gather(result, axes[number], axis=dim, tiled=True)  93.7 us
    all_to_all x1, blocking collectives, sent_to_all(): lax.all_to_all(jnp.broadcast_to(x[None], (size, *x.shape)), axis, 0, 0, t...  29.6 us
    all_to_all x1, waiting for transfers between devices, per_device(): lax.all_to_all(back, ROW_COL, split_axis=0, concat_axis=0, tiled=True)  28.5 us
    all_to_all x1, waiting for transfers between devices, sent_to_all(): lax.all_to_all(jnp.broadcast_to(x[None], (size, *x.shape)), axis, 0, 0, t...  26.2 us
    dot_general x3, matrix products, newton_density(): product = jnp.dot(iterate, factor, preferred_element_type=jnp.float32)  22.3 us
    all_to_all x1, starting transfers between devices, per_device(): lax.all_to_all(outgoing, ROW_COL, split_axis=0, concat_axis=0, tiled=True)  11.9 us
    another operation x3, other arithmetic, per_device(): outgoing = jnp.stack(slots, axis=1)  11.5 us
    another operation x1, local copies, waits for them, and re-layouts, per_device(): outgoing = jnp.stack(slots, axis=1)  10.3 us
  transfers between devices with their start and end apart: 6, of which 4 were waited for; matrix products, arithmetic and copies ran while one was open for 17% of the time, Pallas kernels for 0%

commit v1 on v0

v1 whole, which is shorter than its diff:
```python
import jax
import jax.numpy as jnp
from jax import lax
from jax.experimental import pallas as pl
from jax.experimental.pallas import tpu as pltpu
from jax.sharding import PartitionSpec as P

TILE = 128
MAXT = 8
NB = 32
ROWS = 8
COLS = 16
SUBS = 128
CW = 32
N = MAXT * TILE
RT = NB // ROWS
CT = NB // COLS
F32 = jnp.float32
BF16 = jnp.bfloat16


def kept(pattern, a, b):
    return (pattern[a * NB + b] > 0) | (a == b)


def solve_kernel(ids, lists, orders, pattern, shift, gathered, panel, groups, raw, x, f, d, sems):
    s = ids[1] * ROWS + ids[0]
    order = orders[s]
    potential = shift[0]
    tiles = [lists[s * MAXT + i] for i in range(MAXT)]

    def copy(i, j):
        a, b = tiles[i], tiles[j]
        owner = a // RT * COLS + b // CT
        return pltpu.make_async_copy(
            gathered.at[owner, pl.ds(a % RT * TILE, TILE), pl.ds(b % CT * TILE, TILE)],
            raw.at[pl.ds(i * TILE, TILE), pl.ds(j * TILE, TILE)],
            sems.at[i, j],
        )

    for i in range(MAXT):
        for j in range(MAXT):
            copy(i, j).start()
    rows = lax.broadcasted_iota(jnp.int32, (TILE, TILE), 0)
    cols = lax.broadcasted_iota(jnp.int32, (TILE, TILE), 1)
    eye = jnp.where(rows == cols, 1.0, 0.0).astype(F32)

    def shifted(i, j):
        both = kept(pattern, tiles[i], tiles[j]) & (i < order) & (j < order)
        tile = raw[pl.ds(i * TILE, TILE), pl.ds(j * TILE, TILE)].astype(F32)
        tile = jnp.where(both, tile, 0.0)
        if i == j:
            tile = tile - jnp.where(i < order, potential, 0.0) * eye
        return tile

    largest = jnp.zeros((), F32)
    for i in range(MAXT):
        total = jnp.zeros((TILE, TILE), F32)
        for j in range(MAXT):
            copy(i, j).wait()
            tile = shifted(i, j)
            total = total + tile * tile
        largest = jnp.maximum(largest, jnp.max(jnp.sum(total, axis=1)))
    root = jnp.sqrt(jnp.full((8, TILE), largest + 1e-06, F32))
    inverse = 1.0 / (jnp.abs(potential) + 2.0 * root)
    inverse = inverse[0:1, :]
    for i in range(MAXT):
        for j in range(MAXT):
            x[pl.ds(i * TILE, TILE), pl.ds(j * TILE, TILE)] = (shifted(i, j) * inverse).astype(BF16)

    band = 256
    brow = lax.broadcasted_iota(jnp.int32, (band, N), 0)
    bcol = lax.broadcasted_iota(jnp.int32, (band, N), 1)

    def one(k, _):
        def square(b, _):
            here = pl.ds(pl.multiple_of(b * band, band), band)
            q = jnp.dot(x[here, :], x[...], preferred_element_type=F32)
            diag = jnp.where(brow + b * band == bcol, 1.5, 0.0)
            f[here, :] = (diag - 0.5 * q).astype(BF16)
            return 0

        def apply(b, _):
            here = pl.ds(pl.multiple_of(b * band, band), band)
            y = jnp.dot(x[here, :], f[...], preferred_element_type=F32)
            raw[here, :] = y.astype(BF16)
            return 0

        lax.fori_loop(0, N // band, square, 0)
        lax.fori_loop(0, N // band, apply, 0)
        x[...] = raw[...]
        return 0

    lax.fori_loop(0, 2, one, 0)
    head = pl.ds(0, TILE)
    prow = lax.broadcasted_iota(jnp.int32, (N, TILE), 0)
    pcol = lax.broadcasted_iota(jnp.int32, (N, TILE), 1)
    q = jnp.dot(x[...], x[:, head], preferred_element_type=F32)
    f[:, head] = (jnp.where(prow == pcol, 1.5, 0.0) - 0.5 * q).astype(BF16)
    y = jnp.dot(x[...], f[:, head], preferred_element_type=F32)
    dens = jnp.where(prow == pcol, 0.5, 0.0) - 0.5 * y
    for i in range(MAXT):
        d[:, pl.ds(i * TILE, TILE)] = dens[i * TILE : (i + 1) * TILE, :].T
    offset = pl.multiple_of(s % (TILE // CW) * CW, CW)
    groups[...] = jnp.zeros_like(groups)
    for i in range(MAXT):
        piece = d[pl.ds(offset, CW), pl.ds(i * TILE, TILE)].astype(BF16)
        panel[i] = piece

        @pl.when(i < order)
        def _():
            groups[tiles[i] // CT] = piece


def hp_kernel(ids, lists, orders, pattern, gathered, panels, hp, pt, strip):
    step = pl.program_id(0)

    @pl.when(step == 0)
    def _():
        pt[...] = jnp.zeros_like(pt)
        for k in range(ROWS):
            s = ids[1] * ROWS + k
            for i in range(MAXT):

                @pl.when(i < orders[s])
                def _():
                    where = pl.multiple_of(lists[s * MAXT + i] * TILE, TILE)
                    pt[pl.ds(k * CW, CW), pl.ds(where, TILE)] = panels[k, i]

    for c in range(COLS):
        for i in range(RT):
            for j in range(CT):
                b = c * CT + j
                live = kept(pattern, step * RT + i, b)

                @pl.when(live)
                def _():
                    strip[pl.ds(i * TILE, TILE), pl.ds(b * TILE, TILE)] = gathered[
                        c, pl.ds(i * TILE, TILE), pl.ds(j * TILE, TILE)
                    ]

                @pl.when(jnp.logical_not(live))
                def _():
                    strip[pl.ds(i * TILE, TILE), pl.ds(b * TILE, TILE)] = jnp.zeros(
                        (TILE, TILE), BF16
                    )

    hp[...] = lax.dot_general(
        strip[...], pt[...], (((1,), (1,)), ((), ())), preferred_element_type=F32
    ).astype(BF16)


def final_kernel(ids, present, arrived, hp, density, php, pt):
    def place(s, _):
        owner = s % ROWS * COLS + s // ROWS
        here = pl.ds(pl.multiple_of(s * CW, CW), CW)
        for a in range(RT):
            piece = arrived[owner, a // CT]
            live = present[s * RT + a] > 0
            pt[here, pl.ds(a * TILE, TILE)] = jnp.where(live, piece, jnp.zeros_like(piece))
        return 0

    lax.fori_loop(0, SUBS, place, 0)
    php[...] = lax.dot_general(
        pt[...], hp[...], (((0,), (0,)), ((), ())), preferred_element_type=F32
    )
    width = CT * TILE
    mine = pt[pl.ds(pl.multiple_of(ids[1] * width, width), width), :]
    density[...] = mine.T


def per_device(hamiltonian, pattern, tile_lists, orders, shift):
    row = lax.axis_index("row")
    col = lax.axis_index("col")
    ids = jnp.stack([row, col]).astype(jnp.int32)
    lists = tile_lists.reshape(-1)
    flat_pattern = pattern.reshape(-1)
    smem = pl.BlockSpec(memory_space=pltpu.SMEM)
    vmem = pl.BlockSpec(memory_space=pltpu.VMEM)
    gathered = lax.all_gather(hamiltonian, ("row", "col"), axis=0, tiled=False)
    panel, groups = pl.pallas_call(
        solve_kernel,
        out_shape=(
            jax.ShapeDtypeStruct((MAXT, CW, TILE), BF16),
            jax.ShapeDtypeStruct((NB // CT, CW, TILE), BF16),
        ),
        in_specs=[smem] * 5 + [pl.BlockSpec(memory_space=pl.ANY)],
        out_specs=(vmem, vmem),
        scratch_shapes=[
            pltpu.VMEM((N, N), BF16),
            pltpu.VMEM((N, N), BF16),
            pltpu.VMEM((N, N), BF16),
            pltpu.VMEM((TILE, N), F32),
            pltpu.SemaphoreType.DMA((MAXT, MAXT)),
        ],
        name="solve",
    )(ids, lists, orders, flat_pattern, shift, gathered)
    outgoing = jnp.broadcast_to(
        groups.reshape(ROWS, 1, CT, CW, TILE), (ROWS, COLS, CT, CW, TILE)
    ).reshape(SUBS, CT, CW, TILE)
    arrived = lax.all_to_all(outgoing, ("row", "col"), 0, 0, tiled=True)
    panels = lax.all_gather(panel, "row", axis=0, tiled=False)
    hp = pl.pallas_call(
        hp_kernel,
        out_shape=jax.ShapeDtypeStruct((NB * TILE, CT * TILE), BF16),
        grid_spec=pltpu.PrefetchScalarGridSpec(
            num_scalar_prefetch=4,
            grid=(ROWS,),
            in_specs=[
                pl.BlockSpec((COLS, RT * TILE, CT * TILE), lambda r, *_: (r, 0, 0)),
                pl.BlockSpec((ROWS, MAXT, CW, TILE), lambda r, *_: (0, 0, 0, 0)),
            ],
            out_specs=pl.BlockSpec((RT * TILE, CT * TILE), lambda r, *_: (r, 0)),
            scratch_shapes=[
                pltpu.VMEM((CT * TILE, NB * TILE), BF16),
                pltpu.VMEM((RT * TILE, NB * TILE), BF16),
            ],
        ),
        name="hp",
    )(ids, lists, orders, flat_pattern, gathered, panels)
    own = row * RT + jnp.arange(RT, dtype=jnp.int32)
    live = jnp.arange(MAXT, dtype=jnp.int32)[None, :] < orders[:, None]
    present = jnp.any((tile_lists[:, None, :] == own[None, :, None]) & live[:, None, :], axis=2)
    density, php = pl.pallas_call(
        final_kernel,
        out_shape=(
            jax.ShapeDtypeStruct((RT * TILE, CT * TILE), BF16),
            jax.ShapeDtypeStruct((RT * TILE, CT * TILE), F32),
        ),
        in_specs=[smem, smem, vmem, vmem],
        out_specs=(vmem, vmem),
        scratch_shapes=[pltpu.VMEM((NB * TILE, RT * TILE), BF16)],
        name="final",
    )(ids, present.astype(jnp.int32).reshape(-1), arrived, hp)
    return density, php


def solution(mesh):
    return jax.shard_map(
        per_device,
        mesh=mesh,
        in_specs=(P("row", "col"), P(), P(), P(), P()),
        out_specs=(P("row", "col"), P("row", "col")),
        check_vma=False,
    )
```

time: 319 us -> 231 us (0.72)
  Pallas kernels: 0 us -> 56.7 us
  waiting for transfers between devices: 156 us -> 110 us
  matrix products: 30.9 us -> 0 us
  local copies, waits for them, and re-layouts: 37 us -> 7.79 us
  other arithmetic: 23.9 us -> 0.76 us
  starting transfers between devices: 25.1 us -> 7.28 us
    all_to_all x3 -> x1, waiting for transfers between devices: 61.5 us -> 0.01 us  [per_device(): arrived = lax.all_to_all(outgoing, ('row', 'col'), 0, 0, tiled=True)]
    pallas_call x0 -> x3, Pallas kernels: none -> 56.7 us  [the longest x1 29.5 us: per_device(): pl.pallas_call(hp_kernel, out_shape=jax.ShapeDtypeStruct((NB * TILE, CT *...]
    dot_general x6 -> x0, matrix products: 30.9 us -> none  [the longest x3 22.3 us: newton_density(): product = jnp.dot(iterate, factor, preferred_element_type=jnp.float32)]
    all_gather x0 -> x1, blocking collectives: none -> 30.1 us  [per_device(): panels = lax.all_gather(panel, 'row', axis=0, tiled=False)]
    all_to_all x1 -> x0, blocking collectives: 29.6 us -> none  [sent_to_all(): lax.all_to_all(jnp.broadcast_to(x[None], (size, *x.shape)), axis, 0, 0, t...]
    all_to_all x3 -> x1, starting transfers between devices: 25 us -> 7.24 us  [per_device(): arrived = lax.all_to_all(outgoing, ('row', 'col'), 0, 0, tiled=True)]
    all_gather x3 -> x1, waiting for transfers between devices: 93.7 us -> 109 us  [per_device(): gathered = lax.all_gather(hamiltonian, ('row', 'col'), axis=0, tiled=False)]
    gather x4 -> x0, local copies, waits for them, and re-layouts: 11 us -> none  [the longest x2 6.06 us: per_device(): picked = jnp.take(blocks, which, axis=0)]
  transfers between devices with their start and end apart: 6 -> 2, of which waited for: 4 -> 1; matrix products, arithmetic and copies ran while one was open for 17% -> 2% of each run, Pallas kernels for 0% -> 13%
where the time goes in v1:
time: 231 us; the launch traced here: 227 us
  waiting for transfers between devices  110 us (48%)
  Pallas kernels  56.7 us (25%)
  blocking collectives  30.1 us (13%)
  between operations  14.7 us (6%)
  local copies, waits for them, and re-layouts  7.79 us (3%)
  starting transfers between devices  7.28 us (3%)
    all_gather x1, waiting for transfers between devices, per_device(): gathered = lax.all_gather(hamiltonian, ('row', 'col'), axis=0, tiled=False)  109 us
    all_gather x1, blocking collectives, per_device(): panels = lax.all_gather(panel, 'row', axis=0, tiled=False)  30.1 us
    pallas_call x1, Pallas kernels, per_device(): pl.pallas_call(hp_kernel, out_shape=jax.ShapeDtypeStruct((NB * TILE, CT *...  29.5 us
    pallas_call x1, Pallas kernels, per_device(): pl.pallas_call(solve_kernel, out_shape=(jax.ShapeDtypeStruct((MAXT, CW, T...  20.6 us
    all_to_all x1, starting transfers between devices, per_device(): arrived = lax.all_to_all(outgoing, ('row', 'col'), 0, 0, tiled=True)  7.24 us
    pallas_call x1, Pallas kernels, per_device(): pl.pallas_call(final_kernel, out_shape=(jax.ShapeDtypeStruct((RT * TILE,...  6.67 us
  transfers between devices with their start and end apart: 2, of which 1 were waited for; matrix products, arithmetic and copies ran while one was open for 2% of the time, Pallas kernels for 13%

profile of v1, /device:TPU:1, one launch (start us, length us, event | category | flops | bytes accessed | tf_op | source)
XLA Modules:
  0.0 227.1 jit_solution(9429379753437929338)
XLA Ops:
  7.2 0.0 all-gather.4.cloned.1.call-start
  7.2 0.7 all-gather.4.cloned.1.call-update
  7.9 0.8 copy.13
  8.7 0.7 reshape.41.lists
  9.4 1.4 reshape.42.pattern
  11.4 0.7 pad_add_fusion.ids
  12.1 109.0 %all-gather.4.cloned.1.call-done = bf16[65536,256]{1,0:T(8,128)(2,1)} async-done(((bf16[512,256]{1,0:T(8,128)(2,1)}), bf16[65536,256]{1,0:T(8,128)(2,1)}) %all-gather.4.cloned.1.call-update) | async-done | bytes 33554448 | tf_op jit(solution)/shard_map/all_gather | solution.py:180
  121.1 20.6 %solve.1 = (bf16[8,32,128]{2,1,0:T(8,128)(2,1)}, bf16[16,32,128]{2,1,0:T(8,128)(2,1)}) custom-call(s32[2]{0:T(128)} %pad_add_fusion.ids, s32[1024]{0:T(1024)} %reshape.41.lists, s32[128]{0:T(128)} %orders.3, s32[1024]{0:T(1024)} %reshape.42.pattern, f32[1]{0:T(128)S(6)} %copy.14.shift, bf16[128,512,256]{2,1,0:T(8,128)(2,1)} %bitcast.6), custom_call_target="tpu_custom_call" | custom-call | tf_op jit(solution)/shard_map/solve/pallas_call | solution.py:181
  141.7 2.8 %broadcast_in_dim.5 = bf16[8,16,2,32,128]{4,3,2,1,0:T(8,128)(2,1)} broadcast(bf16[8,2,32,128]{3,2,1,0:T(8,128)(2,1)} %bitcast.10), dimensions={0,2,3,4} | broadcast | bytes 2228224 | tf_op jit(solution)/shard_map/broadcast_in_dim | solution.py:198
  144.4 0.0 copy-start.3
  144.4 0.0 copy-start.2
  144.4 0.0 copy-start.1
  144.4 7.2 %all-to-all-start = ((bf16[128,2,32,128]{3,2,1,0:T(8,128)(2,1)}), bf16[128,2,32,128]{3,2,1,0:T(8,128)(2,1)S(1)}, u32[]{:S(2)}, u32[]{:S(2)}) async-start(bf16[128,2,32,128]{3,2,1,0:T(8,128)(2,1)} %bitcast.8), calls=%async_computation | async-start | bytes 4194304 | tf_op jit(solution)/shard_map/all_to_all | solution.py:201
  151.7 0.0 copy-done.3
  151.7 0.0 copy-done.2
  151.7 0.1 and_reduce_fusion
  151.8 0.1 copy.12
  151.9 0.7 reshape.44.present
  152.6 0.0 copy-done.1
  152.6 30.1 %all-gather.1 = bf16[64,32,128]{2,1,0:T(8,128)(2,1)} all-gather(bf16[8,32,128]{2,1,0:T(8,128)(2,1)S(1)} %copy-done.1), channel_id=3, replica_groups=mesh['row'=8,'col'=16] {'row'}, dimensions={0}, use_global_device_ids=true | all-gather | bytes 589824 | tf_op jit(solution)/shard_map/all_gather | solution.py:202
  182.7 29.5 %hp.1 = bf16[4096,256]{1,0:T(8,128)(2,1)} custom-call(s32[2]{0:T(128)} %pad_add_fusion.ids, s32[1024]{0:T(1024)} %reshape.41.lists, s32[128]{0:T(128)} %orders.3, s32[1024]{0:T(1024)} %reshape.42.pattern, bf16[128,512,256]{2,1,0:T(8,128)(2,1)} %bitcast.7, bf16[8,8,32,128]{3,2,1,0:T(8,128)(2,1)} %bitcast.9), custom_call_target="tpu_custom_call" | custom-call | tf_op jit(solution)/shard_map/hp/pallas_call | solution.py:203
  212.2 0.0 all-to-all-done.arrived
  212.2 0.0 copy-start
  212.2 1.3 copy-done
  213.6 6.7 %final.1 = (bf16[512,256]{1,0:T(8,128)(2,1)}, f32[512,256]{1,0:T(8,128)}) custom-call(s32[2]{0:T(128)} %pad_add_fusion.ids, s32[512]{0:T(512)} %reshape.44.present, bf16[128,2,32,128]{3,2,1,0:T(8,128)(2,1)} %copy-done, bf16[4096,256]{1,0:T(8,128)(2,1)} %hp.1), custom_call_target="tpu_custom_call" | custom-call | tf_op jit(solution)/shard_map/final/pallas_call | solution.py:224
  (3 shorter events, 0.0 us)
Async XLA Ops:
  7.2 113.9 %all-gather.4.cloned.1.call-start = ((), (), s32[]{:S(2)}) async-start(), calls=%async_computation.1 | async-start | bytes 33816576 | tf_op jit(solution)/shard_map/all_gather | solution.py:180
  144.4 7.3 %copy-start.3 = (s32[128]{0:T(128)S(1)}, s32[128]{0:T(128)}, u32[]{:S(2)}) copy-start(s32[128]{0:T(128)} %orders.3) | copy-start | bytes 1540
  144.4 7.3 %copy-start.2 = (s32[128,8]{0,1:T(8,128)S(1)}, s32[128,8]{0,1:T(8,128)}, u32[]{:S(2)}) copy-start(s32[128,8]{0,1:T(8,128)} %param.7) | copy-start | bytes 12292
  144.4 8.2 %copy-start.1 = (bf16[8,32,128]{2,1,0:T(8,128)(2,1)S(1)}, bf16[8,32,128]{2,1,0:T(8,128)(2,1)}, u32[]{:S(2)}) copy-start(bf16[8,32,128]{2,1,0:T(8,128)(2,1)} %get-tuple-element.5) | copy-start | bytes 196612
  144.4 67.8 %all-to-all-start = ((bf16[128,2,32,128]{3,2,1,0:T(8,128)(2,1)}), bf16[128,2,32,128]{3,2,1,0:T(8,128)(2,1)S(1)}, u32[]{:S(2)}, u32[]{:S(2)}) async-start(bf16[128,2,32,128]{3,2,1,0:T(8,128)(2,1)} %bitcast.8), calls=%async_computation | async-start | bytes 4194304 | tf_op jit(solution)/shard_map/all_to_all | solution.py:201
  212.2 1.3 copy-start
Sparse Core Ops, SparseCore 0:
  11.1 109.9 all-gather.3

commit v2 on v1

v2 whole, which is shorter than its diff:
```python
import jax
import jax.numpy as jnp
from jax import lax
from jax.experimental import pallas as pl
from jax.experimental.pallas import tpu as pltpu
from jax.sharding import PartitionSpec as P

TILE = 128
MAXT = 8
NB = 32
ROWS = 8
COLS = 16
SUBS = 128
CW = 32
N = MAXT * TILE
RT = NB // ROWS
CT = NB // COLS
WIDTH = CT * TILE
F32 = jnp.float32
BF16 = jnp.bfloat16


def kept(pattern, a, b):
    return (pattern[a * NB + b] > 0) | (a == b)


def sent_to_all(x, axis, size):
    return lax.all_to_all(jnp.broadcast_to(x[None], (size, *x.shape)), axis, 0, 0, tiled=True)


def pack_kernel(ids, lists, orders, strip, out):
    def one(k, _):
        s = k * ROWS + ids[0]
        half = jnp.int32(-1)
        for j in range(MAXT):
            b = lists[s * MAXT + j]
            half = jnp.where((b // CT == ids[1]) & (j < orders[s]), b % CT, half)

        @pl.when(half >= 0)
        def _():
            lanes = pl.ds(pl.multiple_of(half * TILE, TILE), TILE)
            for i in range(MAXT):
                start = pl.multiple_of(lists[s * MAXT + i] * TILE, TILE)
                out[k, i] = strip[pl.ds(start, TILE), lanes]

        return 0

    lax.fori_loop(0, COLS, one, 0)


def solve_kernel(ids, lists, orders, pattern, shift, tiles, panel, x, f, y, d):
    s = ids[1] * ROWS + ids[0]
    order = orders[s]
    potential = shift[0]
    names = [lists[s * MAXT + j] for j in range(MAXT)]
    rows = lax.broadcasted_iota(jnp.int32, (TILE, TILE), 0)
    cols = lax.broadcasted_iota(jnp.int32, (TILE, TILE), 1)
    eye = jnp.where(rows == cols, 1.0, 0.0).astype(F32)

    def shifted(i, j):
        both = kept(pattern, names[i], names[j]) & (i < order) & (j < order)
        tile = jnp.where(both, tiles[names[j] // CT, i].astype(F32), 0.0)
        if i == j:
            tile = tile - jnp.where(i < order, potential, 0.0) * eye
        return tile

    largest = jnp.zeros((), F32)
    for i in range(MAXT):
        total = jnp.zeros((TILE, TILE), F32)
        for j in range(MAXT):
            tile = shifted(i, j)
            total = total + tile * tile
        largest = jnp.maximum(largest, jnp.max(jnp.sum(total, axis=1)))
    root = jnp.sqrt(jnp.full((8, TILE), largest + 1e-06, F32))
    inverse = (1.0 / (jnp.abs(potential) + 2.0 * root))[0:1, :]
    for i in range(MAXT):
        for j in range(MAXT):
            x[pl.ds(i * TILE, TILE), pl.ds(j * TILE, TILE)] = (shifted(i, j) * inverse).astype(BF16)

    band = 256
    brow = lax.broadcasted_iota(jnp.int32, (band, N), 0)
    bcol = lax.broadcasted_iota(jnp.int32, (band, N), 1)

    def step(source, target):
        def square(b, _):
            here = pl.ds(pl.multiple_of(b * band, band), band)
            q = jnp.dot(source[here, :], source[...], preferred_element_type=F32)
            diag = jnp.where(brow + b * band == bcol, 1.5, 0.0)
            f[here, :] = (diag - 0.5 * q).astype(BF16)
            return 0

        def apply(b, _):
            here = pl.ds(pl.multiple_of(b * band, band), band)
            target[here, :] = jnp.dot(
                source[here, :], f[...], preferred_element_type=F32
            ).astype(BF16)
            return 0

        lax.fori_loop(0, N // band, square, 0)
        lax.fori_loop(0, N // band, apply, 0)

    step(x, y)
    step(y, x)
    head = pl.ds(0, TILE)
    prow = lax.broadcasted_iota(jnp.int32, (N, TILE), 0)
    pcol = lax.broadcasted_iota(jnp.int32, (N, TILE), 1)
    q = jnp.dot(x[...], x[:, head], preferred_element_type=F32)
    f[:, head] = (jnp.where(prow == pcol, 1.5, 0.0) - 0.5 * q).astype(BF16)
    z = jnp.dot(x[...], f[:, head], preferred_element_type=F32)
    dens = jnp.where(prow == pcol, 0.5, 0.0) - 0.5 * z
    for i in range(MAXT):
        d[:, pl.ds(i * TILE, TILE)] = dens[i * TILE : (i + 1) * TILE, :].T
    offset = pl.multiple_of(s % (TILE // CW) * CW, CW)
    for i in range(MAXT):
        panel[i] = d[pl.ds(offset, CW), pl.ds(i * TILE, TILE)].astype(BF16)


def spread_kernel(ids, lists, orders, panels, out):
    out[...] = jnp.zeros_like(out)
    for k in range(ROWS):
        s = ids[1] * ROWS + k
        for i in range(MAXT):
            group = lists[s * MAXT + i] // CT

            @pl.when((i < orders[s]) & (group // (RT // CT) == ids[0]))
            def _():
                for c in range(COLS):
                    out[c, k, group % (RT // CT)] = panels[k, i]


def hp_kernel(ids, lists, orders, pattern, strip, panels, hp, pt, wide, sems):
    copies = [
        pltpu.make_async_copy(strip.at[c], wide.at[:, pl.ds(c * WIDTH, WIDTH)], sems.at[c])
        for c in range(COLS)
    ]
    for copy in copies:
        copy.start()
    pt[...] = jnp.zeros_like(pt)
    for k in range(ROWS):
        s = ids[1] * ROWS + k
        for i in range(MAXT):

            @pl.when(i < orders[s])
            def _():
                where = pl.multiple_of(lists[s * MAXT + i] * TILE, TILE)
                pt[pl.ds(k * CW, CW), pl.ds(where, TILE)] = panels[k, i]

    for copy in copies:
        copy.wait()

    def clear(b, _):
        lanes = pl.ds(pl.multiple_of(b * TILE, TILE), TILE)
        for a in range(RT):

            @pl.when(jnp.logical_not(kept(pattern, ids[0] * RT + a, b)))
            def _():
                wide[pl.ds(a * TILE, TILE), lanes] = jnp.zeros((TILE, TILE), BF16)

        return 0

    lax.fori_loop(0, NB, clear, 0)
    hp[...] = lax.dot_general(
        wide[...], pt[...], (((1,), (1,)), ((), ())), preferred_element_type=F32
    ).astype(BF16)


def final_kernel(ids, present, arrived, hp, density, php, pt):
    def place(s, _):
        here = pl.ds(pl.multiple_of(s * CW, CW), CW)
        for a in range(RT):
            piece = arrived[s, a // CT]
            live = present[s * RT + a] > 0
            pt[here, pl.ds(a * TILE, TILE)] = jnp.where(live, piece, jnp.zeros_like(piece))
        return 0

    lax.fori_loop(0, SUBS, place, 0)
    php[...] = lax.dot_general(
        pt[...], hp[...], (((0,), (0,)), ((), ())), preferred_element_type=F32
    )
    mine = pt[pl.ds(pl.multiple_of(ids[1] * WIDTH, WIDTH), WIDTH), :]
    density[...] = mine.T


def per_device(hamiltonian, pattern, tile_lists, orders, shift):
    row = lax.axis_index("row")
    col = lax.axis_index("col")
    ids = jnp.stack([row, col]).astype(jnp.int32)
    lists = tile_lists.reshape(-1)
    smem = pl.BlockSpec(memory_space=pltpu.SMEM)
    vmem = pl.BlockSpec(memory_space=pltpu.VMEM)
    hbm = pl.BlockSpec(memory_space=pl.ANY)
    flat_pattern = pattern.reshape(-1)
    row_strip = lax.all_gather(hamiltonian, "col", axis=0, tiled=False)
    col_strip = sent_to_all(hamiltonian, "row", ROWS).reshape(NB * TILE, WIDTH)
    packed = pl.pallas_call(
        pack_kernel,
        out_shape=jax.ShapeDtypeStruct((COLS, MAXT, TILE, TILE), BF16),
        in_specs=[smem, smem, smem, vmem],
        out_specs=vmem,
        name="pack",
    )(ids, lists, orders, col_strip)
    tiles = lax.all_to_all(packed, "col", 0, 0, tiled=True)
    panel = pl.pallas_call(
        solve_kernel,
        out_shape=jax.ShapeDtypeStruct((MAXT, CW, TILE), BF16),
        in_specs=[smem] * 5 + [vmem],
        out_specs=vmem,
        scratch_shapes=[
            pltpu.VMEM((N, N), BF16),
            pltpu.VMEM((N, N), BF16),
            pltpu.VMEM((N, N), BF16),
            pltpu.VMEM((TILE, N), F32),
        ],
        name="solve",
    )(ids, lists, orders, flat_pattern, shift, tiles)
    panels = lax.all_gather(panel, "row", axis=0, tiled=False)
    spread = pl.pallas_call(
        spread_kernel,
        out_shape=jax.ShapeDtypeStruct((COLS, ROWS, RT // CT, CW, TILE), BF16),
        in_specs=[smem] * 3 + [vmem],
        out_specs=vmem,
        name="spread",
    )(ids, lists, orders, panels)
    arrived = lax.all_to_all(spread, "col", 0, 0, tiled=True)
    hp = pl.pallas_call(
        hp_kernel,
        out_shape=jax.ShapeDtypeStruct((RT * TILE, WIDTH), BF16),
        in_specs=[smem] * 4 + [hbm, vmem],
        out_specs=vmem,
        scratch_shapes=[
            pltpu.VMEM((WIDTH, NB * TILE), BF16),
            pltpu.VMEM((RT * TILE, NB * TILE), BF16),
            pltpu.SemaphoreType.DMA((COLS,)),
        ],
        name="hp",
    )(ids, lists, orders, flat_pattern, row_strip, panels)
    hp_strip = sent_to_all(hp, "row", ROWS).reshape(NB * TILE, WIDTH)
    own = row * RT + jnp.arange(RT, dtype=jnp.int32)
    live = jnp.arange(MAXT, dtype=jnp.int32)[None, :] < orders[:, None]
    present = jnp.any((tile_lists[:, None, :] == own[None, :, None]) & live[:, None, :], axis=2)
    density, php = pl.pallas_call(
        final_kernel,
        out_shape=(
            jax.ShapeDtypeStruct((RT * TILE, WIDTH), BF16),
            jax.ShapeDtypeStruct((RT * TILE, WIDTH), F32),
        ),
        in_specs=[smem, smem, vmem, vmem],
        out_specs=(vmem, vmem),
        scratch_shapes=[pltpu.VMEM((NB * TILE, RT * TILE), BF16)],
        name="final",
    )(ids, present.astype(jnp.int32).reshape(-1), arrived.reshape(SUBS, RT // CT, CW, TILE), hp_strip)
    return density, php


def solution(mesh):
    return jax.shard_map(
        per_device,
        mesh=mesh,
        in_specs=(P("row", "col"), P(), P(), P(), P()),
        out_specs=(P("row", "col"), P("row", "col")),
        check_vma=False,
    )
```

time: 231 us -> 258 us (1.12)
  waiting for transfers between devices: 110 us -> 148 us
  starting transfers between devices: 7.28 us -> 27.8 us
  Pallas kernels: 56.7 us -> 41.3 us
  blocking collectives: 30.1 us -> 15.6 us
    all_to_all x1 -> x4, waiting for transfers between devices: 0.01 us -> 147 us  [the longest x1 75.7 us: per_device(): tiles = lax.all_to_all(packed, 'col', 0, 0, tiled=True)]
    all_gather x1, waiting for transfers between devices: 109 us -> 0.02 us  [per_device(): row_strip = lax.all_gather(hamiltonian, 'col', axis=0, tiled=False)]
    all_to_all x1 -> x4, starting transfers between devices: 7.24 us -> 27.8 us  [the longest x2 13.5 us: sent_to_all(): lax.all_to_all(jnp.broadcast_to(x[None], (size, *x.shape)), axis, 0, 0, t...]
    pallas_call x2 -> x4, Pallas kernels: 50 us -> 35.1 us  [the longest x1 18.6 us: per_device(): pl.pallas_call(solve_kernel, out_shape=jax.ShapeDtypeStruct((MAXT, CW, TI...]
    all_gather x1, blocking collectives: 30.1 us -> 15.6 us  [per_device(): panels = lax.all_gather(panel, 'row', axis=0, tiled=False)]
  transfers between devices with their start and end apart: 2 -> 5, of which waited for: 1 -> 4; matrix products, arithmetic and copies ran while one was open for 2% -> 1% of each run, Pallas kernels for 13% -> 14%
where the time goes in v2:
time: 258 us; the launch traced here: 257 us
  waiting for transfers between devices  148 us (57%)
  Pallas kernels  41.3 us (16%)
  starting transfers between devices  27.8 us (11%)
  blocking collectives  15.6 us (6%)
  between operations  14.7 us (6%)
  local copies, waits for them, and re-layouts  8.64 us (3%)
    all_to_all x1, waiting for transfers between devices, per_device(): tiles = lax.all_to_all(packed, 'col', 0, 0, tiled=True)  75.7 us
    all_to_all x2, waiting for transfers between devices, sent_to_all(): lax.all_to_all(jnp.broadcast_to(x[None], (size, *x.shape)), axis, 0, 0, t...  49.5 us
    all_to_all x1, waiting for transfers between devices, per_device(): arrived = lax.all_to_all(spread, 'col', 0, 0, tiled=True)  21.8 us
    pallas_call x1, Pallas kernels, per_device(): pl.pallas_call(solve_kernel, out_shape=jax.ShapeDtypeStruct((MAXT, CW, TI...  18.6 us
    all_gather x1, blocking collectives, per_device(): panels = lax.all_gather(panel, 'row', axis=0, tiled=False)  15.6 us
    all_to_all x2, starting transfers between devices, sent_to_all(): lax.all_to_all(jnp.broadcast_to(x[None], (size, *x.shape)), axis, 0, 0, t...  13.5 us
    all_to_all x1, starting transfers between devices, per_device(): arrived = lax.all_to_all(spread, 'col', 0, 0, tiled=True)  7.56 us
    pallas_call x1, Pallas kernels, per_device(): pl.pallas_call(hp_kernel, out_shape=jax.ShapeDtypeStruct((RT * TILE, WIDT...  7.34 us
  transfers between devices with their start and end apart: 5, of which 4 were waited for; matrix products, arithmetic and copies ran while one was open for 1% of the time, Pallas kernels for 14%

profile of v2, /device:TPU:1, one launch (start us, length us, event | category | flops | bytes accessed | tf_op | source)
XLA Modules:
  0.0 256.5 jit_solution(1297537297293283750)
XLA Ops:
  7.2 2.4 broadcast_in_dim.6
  9.6 0.0 copy-start.3
  9.6 6.9 %all-to-all-start = ((bf16[8,512,256]{2,1,0:T(8,128)(2,1)}), bf16[8,512,256]{2,1,0:T(8,128)(2,1)S(1)}, u32[]{:S(2)}, u32[]{:S(2)}) async-start(bf16[8,512,256]{2,1,0:T(8,128)(2,1)} %broadcast_in_dim.6), calls=%async_computation | async-start | bytes 4194304 | tf_op jit(solution)/shard_map/all_to_all | solution.py:28
  16.5 0.0 all-gather.4.cloned.1.call-start
  16.5 0.7 all-gather.4.cloned.1.call-update
  17.2 0.0 copy-done.3
  17.3 0.1 copy.13
  17.4 0.7 reshape.47.lists
  18.0 0.6 pad_add_fusion.ids
  18.7 24.1 %all-to-all-done = bf16[8,512,256]{2,1,0:T(8,128)(2,1)S(1)} async-done(((bf16[8,512,256]{2,1,0:T(8,128)(2,1)}), bf16[8,512,256]{2,1,0:T(8,128)(2,1)S(1)}, u32[]{:S(2)}, u32[]{:S(2)}) %all-to-all-start) | async-done | bytes 2097184 | tf_op jit(solution)/shard_map/all_to_all | solution.py:28
  42.7 0.0 copy-start
  42.7 1.4 copy-done
  44.1 5.1 %pack.1 = bf16[16,8,128,128]{3,2,1,0:T(8,128)(2,1)} custom-call(s32[2]{0:T(128)} %pad_add_fusion.ids, s32[1024]{0:T(1024)} %reshape.47.lists, s32[128]{0:T(128)} %orders.7, bf16[4096,256]{1,0:T(8,128)(2,1)} %bitcast.7), custom_call_target="tpu_custom_call" | custom-call | tf_op jit(solution)/shard_map/pack/pallas_call | solution.py:195
  49.2 0.0 copy-start.2
  49.2 6.8 %all-to-all-start.1 = ((bf16[16,8,128,128]{3,2,1,0:T(8,128)(2,1)}), bf16[16,8,128,128]{3,2,1,0:T(8,128)(2,1)}, u32[]{:S(2)}, u32[]{:S(2)}) async-start(bf16[16,8,128,128]{3,2,1,0:T(8,128)(2,1)} %pack.1), calls=%async_computation.1 | async-start | bytes 8388608 | tf_op jit(solution)/shard_map/all_to_all | solution.py:202
  56.0 0.0 copy-done.2
  56.0 0.7 reshape.48.pattern
  57.3 75.7 %all-to-all-done.1.tiles = bf16[16,8,128,128]{3,2,1,0:T(8,128)(2,1)} async-done(((bf16[16,8,128,128]{3,2,1,0:T(8,128)(2,1)}), bf16[16,8,128,128]{3,2,1,0:T(8,128)(2,1)}, u32[]{:S(2)}, u32[]{:S(2)}) %all-to-all-start.1) | async-done | bytes 4194336 | tf_op jit(solution)/shard_map/all_to_all | solution.py:202
  133.0 18.6 %solve.1 = bf16[8,32,128]{2,1,0:T(8,128)(2,1)} custom-call(s32[2]{0:T(128)} %pad_add_fusion.ids, s32[1024]{0:T(1024)} %reshape.47.lists, s32[128]{0:T(128)} %orders.7, s32[1024]{0:T(1024)} %reshape.48.pattern, f32[1]{0:T(128)S(6)} %copy.14.shift, bf16[16,8,128,128]{3,2,1,0:T(8,128)(2,1)} %all-to-all-done.1.tiles), custom_call_target="tpu_custom_call" | custom-call | tf_op jit(solution)/shard_map/solve/pallas_call | solution.py:203
  151.6 15.6 %all-gather = bf16[64,32,128]{2,1,0:T(8,128)(2,1)} all-gather(bf16[8,32,128]{2,1,0:T(8,128)(2,1)} %solve.1), channel_id=2, replica_groups=mesh['row'=8,'col'=16] {'row'}, dimensions={0}, use_global_device_ids=true | all-gather | bytes 589824 | tf_op jit(solution)/shard_map/all_gather | solution.py:216
  167.2 4.1 %spread.1 = bf16[16,8,2,32,128]{4,3,2,1,0:T(8,128)(2,1)} custom-call(s32[2]{0:T(128)} %pad_add_fusion.ids, s32[1024]{0:T(1024)} %reshape.47.lists, s32[128]{0:T(128)} %orders.7, bf16[8,8,32,128]{3,2,1,0:T(8,128)(2,1)} %bitcast.9), custom_call_target="tpu_custom_call" | custom-call | tf_op jit(solution)/shard_map/spread/pallas_call | solution.py:217
  171.3 7.6 %all-to-all-start.2 = ((bf16[16,8,2,32,128]{4,3,2,1,0:T(8,128)(2,1)}), bf16[16,8,2,32,128]{4,3,2,1,0:T(8,128)(2,1)S(1)}, u32[]{:S(2)}, u32[]{:S(2)}) async-start(bf16[16,8,2,32,128]{4,3,2,1,0:T(8,128)(2,1)} %spread.1), calls=%async_computation.2 | async-start | bytes 4194304 | tf_op jit(solution)/shard_map/all_to_all | solution.py:224
  178.9 0.0 all-gather.4.cloned.1.call-done
  178.9 7.3 %hp.1 = bf16[512,256]{1,0:T(8,128)(2,1)} custom-call(s32[2]{0:T(128)} %pad_add_fusion.ids, s32[1024]{0:T(1024)} %reshape.47.lists, s32[128]{0:T(128)} %orders.7, s32[1024]{0:T(1024)} %reshape.48.pattern, bf16[16,512,256]{2,1,0:T(8,128)(2,1)} %bitcast.11, bf16[8,8,32,128]{3,2,1,0:T(8,128)(2,1)} %bitcast.10), custom_call_target="tpu_custom_call" | custom-call | tf_op jit(solution)/shard_map/hp/pallas_call | solution.py:225
  186.3 21.8 %all-to-all-done.2 = bf16[16,8,2,32,128]{4,3,2,1,0:T(8,128)(2,1)S(1)} async-done(((bf16[16,8,2,32,128]{4,3,2,1,0:T(8,128)(2,1)}), bf16[16,8,2,32,128]{4,3,2,1,0:T(8,128)(2,1)S(1)}, u32[]{:S(2)}, u32[]{:S(2)}) %all-to-all-start.2) | async-done | bytes 2097184 | tf_op jit(solution)/shard_map/all_to_all | solution.py:224
  208.1 0.0 copy-start.1
  208.1 2.6 %broadcast_in_dim.8 = bf16[8,512,256]{2,1,0:T(8,128)(2,1)} broadcast(bf16[512,256]{1,0:T(8,128)(2,1)} %hp.1), dimensions={1,2} | broadcast | bytes 2359296 | tf_op jit(solution)/shard_map/broadcast_in_dim | solution.py:28
  210.7 0.0 copy-start.4
  210.7 0.0 copy-done.1
  210.7 6.5 %all-to-all-start.3 = ((bf16[8,512,256]{2,1,0:T(8,128)(2,1)}), bf16[8,512,256]{2,1,0:T(8,128)(2,1)}, u32[]{:S(2)}, u32[]{:S(2)}) async-start(bf16[8,512,256]{2,1,0:T(8,128)(2,1)} %broadcast_in_dim.8), calls=%async_computation.3 | async-start | bytes 4194304 | tf_op jit(solution)/shard_map/all_to_all | solution.py:28
  217.2 0.0 copy-done.4
  217.2 0.1 and_reduce_fusion
  217.3 0.1 copy.12
  217.5 0.7 reshape.52.present
  218.2 25.4 %all-to-all-done.3 = bf16[8,512,256]{2,1,0:T(8,128)(2,1)} async-done(((bf16[8,512,256]{2,1,0:T(8,128)(2,1)}), bf16[8,512,256]{2,1,0:T(8,128)(2,1)}, u32[]{:S(2)}, u32[]{:S(2)}) %all-to-all-start.3) | async-done | bytes 2097184 | tf_op jit(solution)/shard_map/all_to_all | solution.py:28
  243.6 6.1 %final.1 = (bf16[512,256]{1,0:T(8,128)(2,1)}, f32[512,256]{1,0:T(8,128)}) custom-call(s32[2]{0:T(128)} %pad_add_fusion.ids, s32[512]{0:T(512)} %reshape.52.present, bf16[128,2,32,128]{3,2,1,0:T(8,128)(2,1)} %bitcast.8, bf16[4096,256]{1,0:T(8,128)(2,1)} %bitcast.6.hp), custom_call_target="tpu_custom_call" | custom-call | tf_op jit(solution)/shard_map/final/pallas_call | solution.py:241
  (3 shorter events, 0.0 us)
Async XLA Ops:
  9.6 7.7 %copy-start.3 = (s32[128,8]{0,1:T(8,128)S(1)}, s32[128,8]{0,1:T(8,128)}, u32[]{:S(2)}) copy-start(s32[128,8]{0,1:T(8,128)} %param.7) | copy-start | bytes 12292
  9.6 33.1 %all-to-all-start = ((bf16[8,512,256]{2,1,0:T(8,128)(2,1)}), bf16[8,512,256]{2,1,0:T(8,128)(2,1)S(1)}, u32[]{:S(2)}, u32[]{:S(2)}) async-start(bf16[8,512,256]{2,1,0:T(8,128)(2,1)} %broadcast_in_dim.6), calls=%async_computation | async-start | bytes 4194304 | tf_op jit(solution)/shard_map/all_to_all | solution.py:28
  16.5 162.4 %all-gather.4.cloned.1.call-start = ((), (), s32[]{:S(2)}) async-start(), calls=%async_computation.4 | async-start | bytes 4456448 | tf_op jit(solution)/shard_map/all_gather | solution.py:193
  42.7 1.4 copy-start
  49.2 6.8 %copy-start.2 = (s32[32,32]{1,0:T(8,128)S(1)}, s32[32,32]{1,0:T(8,128)}, u32[]{:S(2)}) copy-start(s32[32,32]{1,0:T(8,128)} %param.6) | copy-start | bytes 12292
  49.2 83.8 %all-to-all-start.1 = ((bf16[16,8,128,128]{3,2,1,0:T(8,128)(2,1)}), bf16[16,8,128,128]{3,2,1,0:T(8,128)(2,1)}, u32[]{:S(2)}, u32[]{:S(2)}) async-start(bf16[16,8,128,128]{3,2,1,0:T(8,128)(2,1)} %pack.1), calls=%async_computation.1 | async-start | bytes 8388608 | tf_op jit(solution)/shard_map/all_to_all | solution.py:202
  171.3 36.8 %all-to-all-start.2 = ((bf16[16,8,2,32,128]{4,3,2,1,0:T(8,128)(2,1)}), bf16[16,8,2,32,128]{4,3,2,1,0:T(8,128)(2,1)S(1)}, u32[]{:S(2)}, u32[]{:S(2)}) async-start(bf16[16,8,2,32,128]{4,3,2,1,0:T(8,128)(2,1)} %spread.1), calls=%async_computation.2 | async-start | bytes 4194304 | tf_op jit(solution)/shard_map/all_to_all | solution.py:224
  208.1 2.6 %copy-start.1 = (bf16[16,8,2,32,128]{4,3,2,1,0:T(8,128)(2,1)}, bf16[16,8,2,32,128]{4,3,2,1,0:T(8,128)(2,1)S(1)}, u32[]{:S(2)}) copy-start(bf16[16,8,2,32,128]{4,3,2,1,0:T(8,128)(2,1)S(1)} %all-to-all-done.2) | copy-start | bytes 6291460
  210.7 6.5 %copy-start.4 = (s32[128]{0:T(128)S(1)}, s32[128]{0:T(128)}, u32[]{:S(2)}) copy-start(s32[128]{0:T(128)} %orders.7) | copy-start | bytes 1540
  210.7 32.9 %all-to-all-start.3 = ((bf16[8,512,256]{2,1,0:T(8,128)(2,1)}), bf16[8,512,256]{2,1,0:T(8,128)(2,1)}, u32[]{:S(2)}, u32[]{:S(2)}) async-start(bf16[8,512,256]{2,1,0:T(8,128)(2,1)} %broadcast_in_dim.8), calls=%async_computation.3 | async-start | bytes 4194304 | tf_op jit(solution)/shard_map/all_to_all | solution.py:28
Sparse Core Ops, SparseCore 0:
  19.5 87.1 all-gather.3
